TPU v7x, 128 devices: a whole 4x4x4 slice. The times are simulated.
128 devices in a mesh: own: 32 (over x, z, core), rep: 4 (over y).
Axes of the slice: x: 4, y: 4, z: 4, core: 2. Of those that a mesh axis runs over, the one named last changes fastest.
Arguments:
- block_pool: bfloat16 [8192, 64, 576], P(('own', 'rep')), may hold values from -16 to 16
- sel_index: int32 [4096], P(('own', 'rep')), may hold values from 0 to 63
- sel_layer: int32 [4096], P(('own', 'rep')), may hold values from 0 to 15, as said below
- counts: int32 [128], P(('own', 'rep')), may hold values from 8 to 32, as said below
Outputs:
- quant_codes: bfloat16 [32, 4, 32, 8, 18432], P('own', 'rep')
- quant_steps: float32 [32, 288], P('own')
- clip_error: float32 [32, 288], P('own')
Inputs may be any that keep to these rules, and one draw needn't show every extreme that they name: `sel_layer`: among the 32 entries of one device, at most 8 name any one layer; the first 8 entries of every device all name one and the same layer. `counts`: some device has all 32 entries live.
All inputs are finite; a program needn't handle non-finite values.
Results may differ from a plain program's by a relative error of at most 0.001.
Values may be sent and summed in bfloat16 or wider, within the bound.
A program may use at most 128 MiB of HBM per device.

v0:
```python
import jax
import jax.numpy as jnp
from jax import lax
from jax.sharding import PartitionSpec as P

SLICES = 2


headroom = 0.5


def sent_to_all(x, axis):
    count = lax.axis_size(axis)
    return lax.all_to_all(jnp.broadcast_to(x[None], (count, *x.shape)), axis, 0, 0, tiled=True)


def of_everyone(x, axis):
    return sent_to_all(x, axis).max(axis=0)


def over_copies(x, axis):
    everything = sent_to_all(x, axis)
    return jnp.sum(everything, axis=0)


def slot_table(index_row, layer_row, live_count, group_layer, capacity):
    n_select = index_row.shape[0]
    is_live = jnp.arange(n_select) < live_count
    matches = (layer_row[None, :] == group_layer[:, None]) & is_live[None, :]
    ranking = jnp.cumsum(matches.astype(jnp.int32), axis=1) - 1
    slot_hit = matches[:, None, :] & (ranking[:, None, :] == jnp.arange(capacity)[None, :, None])
    chosen = jnp.sum(jnp.where(slot_hit, index_row[None, None, :], 0), axis=2)
    filled = jnp.any(slot_hit, axis=2)
    return (chosen, filled)


def body(block_pool, sel_index, sel_layer, counts):
    own_count = lax.axis_size("own")
    rep_count = lax.axis_size("rep")
    n_select = sel_index.shape[0]
    capacity = n_select // 4
    block_tokens = block_pool.shape[1]
    latent_width = block_pool.shape[2]
    half_width = latent_width // SLICES
    flat_width = block_tokens * half_width
    layer_count = own_count // SLICES
    layer_ids = jnp.arange(layer_count)
    chosen, filled = slot_table(sel_index, sel_layer, counts[0], layer_ids, capacity)
    pool_rows = block_pool.reshape(block_pool.shape[0], block_tokens * latent_width)
    picked = jnp.take(pool_rows, chosen.reshape(-1), axis=0)
    picked = jnp.where(filled.reshape(-1)[:, None], picked, jnp.zeros((), picked.dtype))
    picked = picked.reshape(layer_count, capacity, block_tokens, SLICES, half_width)
    parted = picked.transpose(0, 3, 1, 2, 4).reshape(own_count, capacity, flat_width)
    denominator = float(own_count * rep_count * capacity * block_tokens)
    arrived = lax.all_to_all(parted, "own", split_axis=0, concat_axis=0, tiled=True)
    flat_peak = jnp.max(jnp.abs(arrived), axis=(0, 1)).astype(jnp.float32)
    local_peak = jnp.max(flat_peak.reshape(block_tokens, half_width), axis=0)
    peak_abs = of_everyone(local_peak, "rep")
    step_size = headroom * jnp.maximum(peak_abs, 1.0) / 127.0
    step_flat = jnp.tile(step_size, block_tokens)
    values = arrived.astype(jnp.float32)
    encoded = jnp.clip(values / step_flat, -127.0, 127.0).astype(jnp.bfloat16)
    encoded = lax.optimization_barrier(encoded)
    decoded = encoded.astype(jnp.float32) * step_flat
    flat_error = jnp.sum((values - decoded) ** 2, axis=(0, 1))
    sq_error = jnp.sum(flat_error.reshape(block_tokens, half_width), axis=0)
    error_all = over_copies(sq_error, "rep")
    steps_out = step_size[None, :]
    error_out = (error_all / (step_size * step_size * denominator))[None, :]
    return (encoded[None, None], steps_out, error_out)


def solution(mesh):
    return jax.shard_map(
        body,
        mesh=mesh,
        in_specs=(
            P(("own", "rep"), None, None),
            P(("own", "rep")),
            P(("own", "rep")),
            P(("own", "rep")),
        ),
        out_specs=(P("own", "rep", None, None, None), P("own", None), P("own", None)),
        check_vma=False,
    )
```

profile of v0, /device:TPU:0, one launch (start us, length us, event | category | flops | bytes accessed | tf_op | source)
XLA Modules:
  0.0 263.0 jit_solution(13616483861530412258)
XLA Ops:
  1.3 0.7 fusion.7
  2.0 0.2 reduce_window_sum.11
  2.1 0.4 fusion.6
  2.5 1.0 select_reduce_fusion
  3.5 0.1 reshape.175
  3.7 9.9 %reshape.174 = bf16[64,36864]{1,0:T(8,128)(2,1)} reshape(bf16[64,64,576]{2,1,0:T(8,128)(2,1)} %param.4) | data formatting | bytes 9437184 | tf_op jit(solution)/shard_map/reshape | solution.py:49
  13.6 21.4 %gather_fusion = bf16[128,36864]{1,0:T(8,128)(2,1)} fusion(bf16[64,36864]{1,0:T(8,128)(2,1)} %reshape.174, s32[1024]{0:T(1024)S(1)} %pad_clamp_fusion), kind=kCustom, calls=%fused_computation | custom fusion | bytes 18874880 | tf_op jit(solution)/shard_map/jit(_take)/gather | solution.py:50
  35.0 24.6 %gather.7 = bf16[16,8,64,2,288]{4,3,2,1,0:T(2,128)(2,1)} reshape(bf16[128,36864]{1,0:T(8,128)(2,1)} %gather_fusion) | data formatting | bytes 18874368 | tf_op jit(solution)/shard_map/jit(_take)/gather | solution.py:50
  59.6 16.3 %fusion.4 = bf16[16,2,8,64,288]{4,1,3,2,0:T(2,128)(2,1)S(1)} fusion(pred[16,8]{1,0:T(8,128)(4,1)S(1)} %fusion.6, bf16[16,8,64,2,288]{4,3,2,1,0:T(2,128)(2,1)} %gather.7, pred[16,8]{1,0:T(8,128)(4,1)S(1)} %compare_and_fusion), kind=kLoop, calls=%fused_computation.9 | loop fusion | flops 9437184 | bytes 18874624 | tf_op jit(solution)/shard_map/transpose | solution.py:53
  75.9 6.8 %copy.10 = bf16[16,2,8,64,288]{4,3,2,1,0:T(8,128)(2,1)} copy(bf16[16,2,8,64,288]{4,1,3,2,0:T(2,128)(2,1)S(1)} %fusion.4) | data formatting | bytes 18874368 | tf_op jit(solution)/shard_map/transpose | solution.py:53
  82.7 20.9 %reshape.176 = bf16[32,8,18432]{2,1,0:T(8,128)(2,1)} reshape(bf16[16,2,8,64,288]{4,3,2,1,0:T(8,128)(2,1)} %copy.10) | data formatting | bytes 18874368 | tf_op jit(solution)/shard_map/reshape | solution.py:53
  103.6 114.9 %all_to_all.17 = bf16[32,8,18432]{2,1,0:T(8,128)(2,1)S(1)} all-to-all(bf16[32,8,18432]{2,1,0:T(8,128)(2,1)} %reshape.176), channel_id=1, replica_groups=mesh['own'=32,'rep'=4] {'own'}, dimensions={0} | all-to-all | bytes 18874368 | tf_op jit(solution)/shard_map/all_to_all | solution.py:55
  218.6 0.0 copy-start
  218.6 3.6 %copy-done = bf16[32,8,18432]{2,1,0:T(8,128)(2,1)} copy-done((bf16[32,8,18432]{2,1,0:T(8,128)(2,1)}, bf16[32,8,18432]{2,1,0:T(8,128)(2,1)S(1)}, u32[]{:S(2)}) %copy-start) | copy-done | bytes 9437208
  222.2 1.1 abs_reduce_fusion
  223.3 0.1 reduce_max.35
  223.4 9.6 %all_to_all.18 = f32[4,1,288]{2,1,0:T(1,128)S(1)} all-to-all(f32[4,1,288]{2,1,0:T(1,128)S(1)} %broadcast_in_dim.64), channel_id=1, replica_groups=mesh['own'=32,'rep'=4] {'rep'}, dimensions={0} | all-to-all | bytes 9216 | tf_op jit(solution)/shard_map/all_to_all | solution.py:14
  233.1 0.1 div.30
  233.2 9.8 %fusion.1 = bf16[32,8,18432]{2,1,0:T(8,128)(2,1)} fusion(bf16[32,8,18432]{2,1,0:T(8,128)(2,1)} %copy-done, f32[18432]{0:T(1024)S(1)} %div.30), kind=kLoop, calls=%fused_computation.6 | loop fusion | flops 18874368 | bytes 18948096 | tf_op jit(solution)/shard_map/convert_element_type | solution.py:62
  243.0 10.1 %fusion.3 = f32[18432]{0:T(1024)S(1)} fusion(bf16[32,8,18432]{2,1,0:T(8,128)(2,1)} %copy-done, bf16[32,8,18432]{2,1,0:T(8,128)(2,1)} %fusion.1, f32[18432]{0:T(1024)S(1)} %div.30), kind=kLoop, calls=%fused_computation.8 | loop fusion | flops 28293120 | bytes 19021824 | tf_op jit(solution)/shard_map/reduce_sum | solution.py:65
  253.2 0.1 reshape.177
  253.3 0.6 broadcast_in_dim.66
  253.9 3.2 %all-to-all-start.2 = ((f32[4,1,288]{2,1,0:T(1,128)}), f32[4,1,288]{2,1,0:T(1,128)S(1)}, u32[]{:S(2)}, u32[]{:S(2)}) async-start(f32[4,1,288]{2,1,0:T(1,128)} %broadcast_in_dim.66), calls=%async_computation.2 | async-start | bytes 12288 | tf_op jit(solution)/shard_map/all_to_all | solution.py:14
  257.1 0.6 div.33
  257.7 4.7 %all-to-all-done.2 = f32[4,1,288]{2,1,0:T(1,128)S(1)} async-done(((f32[4,1,288]{2,1,0:T(1,128)}), f32[4,1,288]{2,1,0:T(1,128)S(1)}, u32[]{:S(2)}, u32[]{:S(2)}) %all-to-all-start.2) | async-done | bytes 4640 | tf_op jit(solution)/shard_map/all_to_all | solution.py:14
  262.4 0.6 multiply_divide_fusion
  (12 shorter events, 0.2 us)
Async XLA Ops:
  218.6 3.6 %copy-start = (bf16[32,8,18432]{2,1,0:T(8,128)(2,1)}, bf16[32,8,18432]{2,1,0:T(8,128)(2,1)S(1)}, u32[]{:S(2)}) copy-start(bf16[32,8,18432]{2,1,0:T(8,128)(2,1)S(1)} %all_to_all.17) | copy-start | bytes 28311556
  253.9 8.5 %all-to-all-start.2 = ((f32[4,1,288]{2,1,0:T(1,128)}), f32[4,1,288]{2,1,0:T(1,128)S(1)}, u32[]{:S(2)}, u32[]{:S(2)}) async-start(f32[4,1,288]{2,1,0:T(1,128)} %broadcast_in_dim.66), calls=%async_computation.2 | async-start | bytes 12288 | tf_op jit(solution)/shard_map/all_to_all | solution.py:14
where the time goes:
time: 264 us; the launch traced here: 263 us
  blocking collectives  125 us (47%)
  local copies, waits for them, and re-layouts  88.9 us (34%)
  other arithmetic  40.3 us (15%)
  waiting for transfers between devices  4.71 us (2%)
  starting transfers between devices  3.25 us (1%)
    all_to_all x1, blocking collectives, body(): lax.all_to_all(parted, 'own', split_axis=0, concat_axis=0, tiled=True)  115 us
    gather x2, local copies, waits for them, and re-layouts, body(): picked = jnp.take(pool_rows, chosen.reshape(-1), axis=0)  46 us
    reshape x1, local copies, waits for them, and re-layouts, body(): picked.transpose(0, 3, 1, 2, 4).reshape(own_count, capacity, flat_width)  20.9 us
    transpose x1, other arithmetic, body(): picked.transpose(0, 3, 1, 2, 4).reshape(own_count, capacity, flat_width)  16.3 us
    reduce_sum x1, other arithmetic, body(): flat_error = jnp.sum((values - decoded) ** 2, axis=(0, 1))  10.1 us
    reshape x1, local copies, waits for them, and re-layouts, body(): block_pool.reshape(block_pool.shape[0], block_tokens * latent_width)  9.91 us
    convert_element_type x1, other arithmetic, body(): encoded = jnp.clip(values / step_flat, -127.0, 127.0).astype(jnp.bfloat16)  9.83 us
    all_to_all x1, blocking collectives, sent_to_all(): lax.all_to_all(jnp.broadcast_to(x[None], (count, *x.shape)), axis, 0, 0,...  9.57 us
  transfers between devices with their start and end apart: 1, of which 1 were waited for; matrix products, arithmetic and copies ran while one was open for 0% of the time, Pallas kernels for 0%

commit v1 on v0

v1 whole, which is shorter than its diff:
```python
import functools
import jax
import jax.numpy as jnp
from jax import lax
from jax.experimental import pallas as pl
from jax.experimental.pallas import tpu as pltpu
from jax.sharding import PartitionSpec as P

HEADROOM = 0.5
HALF = 288
PIECE = 4 * HALF
TOK = 64
STEP_TOK = 16
CAP = 8
LAYERS = 16
SEL = 32
DENOM = 32.0 * 4.0 * 8.0 * 64.0


def flatten_kernel(idx_ref, layer_ref, count_ref, pool_ref, out_ref, blocks, picks, seen, sems):
    step = pl.program_id(0)
    rows = STEP_TOK * LAYERS * CAP
    cols = SEL * STEP_TOK

    @pl.when(step == 0)
    def _():
        for j in range(SEL):
            pltpu.make_async_copy(pool_ref.at[idx_ref[j]], blocks.at[j], sems.at[j]).start()
        for layer in range(LAYERS):
            seen[layer] = 0
        col = lax.broadcasted_iota(jnp.int32, (1, cols), 1)
        key = jnp.full((1, cols), -1, jnp.int32)
        live = count_ref[0]
        for j in range(SEL):
            layer = layer_ref[j]
            rank = seen[layer]
            seen[layer] = rank + 1
            slot = jnp.where(j < live, layer * CAP + rank, -1)
            key = jnp.where(col // STEP_TOK == j, slot, key)
        row = lax.broadcasted_iota(jnp.int32, (rows, cols), 0)
        hit = (row % (LAYERS * CAP) == key) & (row // (LAYERS * CAP) == col % STEP_TOK)
        picks[...] = jnp.where(hit, 1.0, 0.0).astype(jnp.bfloat16)
        for j in range(SEL):
            pltpu.make_async_copy(pool_ref.at[idx_ref[j]], blocks.at[j], sems.at[j]).wait()

    start = pl.multiple_of(step * STEP_TOK, STEP_TOK)
    data = blocks[:, pl.ds(start, STEP_TOK), :].reshape(cols, 2 * HALF)
    slots = LAYERS * CAP
    for part in range(STEP_TOK // 4):
        moved = jnp.dot(picks[part * 4 * slots:(part + 1) * 4 * slots, :], data, preferred_element_type=jnp.float32)
        for half in range(2):
            lanes = [moved[t * slots:(t + 1) * slots, half * HALF:(half + 1) * HALF] for t in range(4)]
            flat = jnp.concatenate(lanes, axis=1).astype(jnp.bfloat16)
            out_ref[:, half, :, part * PIECE:(part + 1) * PIECE] = flat.reshape(LAYERS, CAP, PIECE)


def flatten(block_pool, sel_index, sel_layer, counts):
    smem = pl.BlockSpec(memory_space=pltpu.SMEM)
    return pl.pallas_call(
        flatten_kernel,
        grid=(TOK // STEP_TOK,),
        out_shape=jax.ShapeDtypeStruct((LAYERS, 2, CAP, TOK * HALF), jnp.bfloat16),
        in_specs=[smem, smem, smem, pl.BlockSpec(memory_space=pl.ANY)],
        out_specs=pl.BlockSpec((LAYERS, 2, CAP, STEP_TOK * HALF), lambda i: (0, 0, 0, i)),
        scratch_shapes=[
            pltpu.VMEM((SEL, TOK, 2 * HALF), jnp.bfloat16),
            pltpu.VMEM((STEP_TOK * LAYERS * CAP, SEL * STEP_TOK), jnp.bfloat16),
            pltpu.SMEM((LAYERS,), jnp.int32),
            pltpu.SemaphoreType.DMA((SEL,)),
        ],
        compiler_params=pltpu.CompilerParams(dimension_semantics=("arbitrary",), vmem_limit_bytes=48 << 20),
        name="flatten",
    )(sel_index, sel_layer, counts, block_pool)


def rep_exchange(value, inbox, send_sems, recv_sems):
    reps = lax.axis_size("rep")
    me = lax.axis_index("rep")
    inbox[0] = value
    copies = []
    for k in range(1, reps):
        copies.append(pltpu.make_async_remote_copy(
            src_ref=inbox.at[0], dst_ref=inbox.at[k],
            send_sem=send_sems.at[k], recv_sem=recv_sems.at[k],
            device_id={"rep": lax.rem(me + k, reps)}, device_id_type=pl.DeviceIdType.MESH))
    for copy in copies:
        copy.start()
    for copy in copies:
        copy.wait()


def rep_barrier_signal():
    reps = lax.axis_size("rep")
    me = lax.axis_index("rep")
    barrier = pltpu.get_barrier_semaphore()
    for k in range(1, reps):
        pl.semaphore_signal(barrier, inc=1, device_id={"rep": lax.rem(me + k, reps)},
                            device_id_type=pl.DeviceIdType.MESH)
    return barrier


def fold4(row):
    return [row[:, k * HALF:(k + 1) * HALF] for k in range(4)]


def peak_kernel(got_ref, steps_ref, inbox, send_sems, recv_sems):
    barrier = rep_barrier_signal()
    rows = got_ref.shape[0]

    def chunk(i, peak):
        at = pl.multiple_of(i * 16, 16)
        for q in range(TOK // 4):
            part = jnp.abs(got_ref[pl.ds(at, 16), q * PIECE:(q + 1) * PIECE])
            peak = jnp.maximum(peak, part)
        return peak

    peak = lax.fori_loop(0, rows // 16, chunk, jnp.zeros((16, PIECE), jnp.bfloat16))
    row = jnp.max(peak.astype(jnp.float32), axis=0, keepdims=True)
    a, b, c, d = fold4(row)
    row = jnp.maximum(jnp.maximum(a, b), jnp.maximum(c, d))
    pl.semaphore_wait(barrier, 3)
    rep_exchange(jnp.concatenate([row, row[:, :384 - HALF]], axis=1), inbox, send_sems, recv_sems)
    top = jnp.maximum(jnp.maximum(inbox[0], inbox[1]), jnp.maximum(inbox[2], inbox[3]))
    steps_ref[...] = HEADROOM * jnp.maximum(top[:, :HALF], 1.0) / 127.0


def small_scratch():
    return [
        pltpu.VMEM((4, 1, 384), jnp.float32),
        pltpu.SemaphoreType.DMA((4,)),
        pltpu.SemaphoreType.DMA((4,)),
    ]


def peak_steps(got):
    vmem = pl.BlockSpec(memory_space=pltpu.VMEM)
    return pl.pallas_call(
        peak_kernel,
        out_shape=jax.ShapeDtypeStruct((1, HALF), jnp.float32),
        in_specs=[vmem], out_specs=vmem,
        scratch_shapes=small_scratch(),
        compiler_params=pltpu.CompilerParams(collective_id=0, has_side_effects=True, vmem_limit_bytes=24 << 20),
        name="peak_steps",
    )(got)


def error_kernel(sums_ref, out_ref, inbox, send_sems, recv_sems):
    barrier = rep_barrier_signal()
    pl.semaphore_wait(barrier, 3)
    rep_exchange(sums_ref[...], inbox, send_sems, recv_sems)
    total = (inbox[0] + inbox[1]) + (inbox[2] + inbox[3])
    out_ref[...] = total[:, :HALF] * (1.0 / DENOM)


def error_mean(sums):
    vmem = pl.BlockSpec(memory_space=pltpu.VMEM)
    return pl.pallas_call(
        error_kernel,
        out_shape=jax.ShapeDtypeStruct((1, HALF), jnp.float32),
        in_specs=[vmem], out_specs=vmem,
        scratch_shapes=small_scratch(),
        compiler_params=pltpu.CompilerParams(collective_id=1, has_side_effects=True),
        name="error_mean",
    )(sums)


ENC_ROWS = 32


def encode_kernel(got_ref, steps_ref, codes_ref, sums_ref, inv_ref, acc_ref):
    step = pl.program_id(0)

    @pl.when(step == 0)
    def _():
        inv = 1.0 / steps_ref[...]
        inv_ref[...] = jnp.broadcast_to(jnp.concatenate([inv] * 4, axis=1), inv_ref.shape)
        acc_ref[...] = jnp.zeros_like(acc_ref)

    for q in range(TOK // 4):
        lanes = slice(q * PIECE, (q + 1) * PIECE)
        scaled = got_ref[:, lanes].astype(jnp.float32).reshape(ENC_ROWS // 8, 8, PIECE) * inv_ref[...][None]
        code = jnp.clip(scaled, -127.0, 127.0).astype(jnp.bfloat16)
        gap = scaled - code.astype(jnp.float32)
        codes_ref[:, lanes] = code.reshape(ENC_ROWS, PIECE)
        acc_ref[...] += jnp.sum(gap * gap, axis=0)

    @pl.when(step == pl.num_programs(0) - 1)
    def _():
        row = jnp.sum(acc_ref[...], axis=0, keepdims=True)
        a, b, c, d = fold4(row)
        row = (a + b) + (c + d)
        sums_ref[...] = jnp.concatenate([row, row[:, :384 - HALF]], axis=1)


def encode(got, steps):
    rows = got.shape[0]
    return pl.pallas_call(
        encode_kernel,
        grid=(rows // ENC_ROWS,),
        out_shape=(jax.ShapeDtypeStruct(got.shape, jnp.bfloat16), jax.ShapeDtypeStruct((1, 384), jnp.float32)),
        in_specs=[pl.BlockSpec((ENC_ROWS, TOK * HALF), lambda i: (i, 0)), pl.BlockSpec((1, HALF), lambda i: (0, 0))],
        out_specs=(pl.BlockSpec((ENC_ROWS, TOK * HALF), lambda i: (i, 0)), pl.BlockSpec((1, 384), lambda i: (0, 0))),
        scratch_shapes=[pltpu.VMEM((8, PIECE), jnp.float32), pltpu.VMEM((8, PIECE), jnp.float32)],
        compiler_params=pltpu.CompilerParams(dimension_semantics=("arbitrary",), vmem_limit_bytes=24 << 20),
        name="encode",
    )(got, steps)


def body(block_pool, sel_index, sel_layer, counts):
    parted = flatten(block_pool, sel_index, sel_layer, counts).reshape(2 * LAYERS, CAP, TOK * HALF)
    got = lax.all_to_all(parted, "own", split_axis=0, concat_axis=0, tiled=True)
    got = got.reshape(2 * LAYERS * CAP, TOK * HALF)
    steps = peak_steps(got)
    codes, sums = encode(got, steps)
    error = error_mean(sums)
    return codes.reshape(1, 1, 2 * LAYERS, CAP, TOK * HALF), steps, error


def solution(mesh):
    return jax.shard_map(
        body,
        mesh=mesh,
        in_specs=(
            P(("own", "rep"), None, None),
            P(("own", "rep")),
            P(("own", "rep")),
            P(("own", "rep")),
        ),
        out_specs=(P("own", "rep", None, None, None), P("own", None), P("own", None)),
        check_vma=False,
    )
```

time: 264 us -> 158 us (0.60)
  local copies, waits for them, and re-layouts: 88.9 us -> 6.14 us
  other arithmetic: 40.3 us -> 0 us
  Pallas kernels: 0 us -> 34.8 us
  blocking collectives: 125 us -> 115 us
  waiting for transfers between devices: 4.71 us -> 0 us
  starting transfers between devices: 3.25 us -> 0 us
    gather x2 -> x0, local copies, waits for them, and re-layouts: 46 us -> none  [body(): picked = jnp.take(pool_rows, chosen.reshape(-1), axis=0)]
    pallas_call x0 -> x4, Pallas kernels: none -> 34.8 us  [the longest x1 14.3 us: flatten(): pl.pallas_call(flatten_kernel, grid=(TOK // STEP_TOK,), out_shape=jax.Sha...]
    reshape x4 -> x0, local copies, waits for them, and re-layouts: 31 us -> none  [the longest x1 20.9 us: body(): picked.transpose(0, 3, 1, 2, 4).reshape(own_count, capacity, flat_width)]
    transpose x1 -> x0, other arithmetic: 16.3 us -> none  [body(): picked.transpose(0, 3, 1, 2, 4).reshape(own_count, capacity, flat_width)]
    reduce_sum x4 -> x0, other arithmetic: 11.2 us -> none  [the longest x1 10.1 us: body(): flat_error = jnp.sum((values - decoded) ** 2, axis=(0, 1))]
    convert_element_type x1 -> x0, other arithmetic: 9.83 us -> none  [body(): encoded = jnp.clip(values / step_flat, -127.0, 127.0).astype(jnp.bfloat16)]
    all_to_all x2 -> x1, blocking collectives: 125 us -> 115 us  [body(): got = lax.all_to_all(parted, 'own', split_axis=0, concat_axis=0, tiled=True)]
    transpose x1 -> x0, local copies, waits for them, and re-layouts: 6.85 us -> none  [body(): picked.transpose(0, 3, 1, 2, 4).reshape(own_count, capacity, flat_width)]
  transfers between devices with their start and end apart: 1 -> 0, of which waited for: 1 -> 0; matrix products, arithmetic and copies ran while one was open for 0% -> 0% of each run, Pallas kernels for 0% -> 0%
where the time goes in v1:
time: 158 us; the launch traced here: 157 us
  blocking collectives  115 us (73%)
  Pallas kernels  34.8 us (22%)
  local copies, waits for them, and re-layouts  6.14 us (4%)
    all_to_all x1, blocking collectives, body(): got = lax.all_to_all(parted, 'own', split_axis=0, concat_axis=0, tiled=True)  115 us
    pallas_call x1, Pallas kernels, flatten(): pl.pallas_call(flatten_kernel, grid=(TOK // STEP_TOK,), out_shape=jax.Sha...  14.3 us
    pallas_call x1, Pallas kernels, encode(): pl.pallas_call(encode_kernel, grid=(rows // ENC_ROWS,), out_shape=(jax.Sh...  7.98 us
    pallas_call x1, Pallas kernels, error_mean(): pl.pallas_call(error_kernel, out_shape=jax.ShapeDtypeStruct((1, HALF), jn...  6.43 us
    unnamed x10, local copies, waits for them, and re-layouts  6.14 us
    pallas_call x1, Pallas kernels, peak_steps(): pl.pallas_call(peak_kernel, out_shape=jax.ShapeDtypeStruct((1, HALF), jnp...  6.14 us

profile of v1, /device:TPU:0, one launch (start us, length us, event | category | flops | bytes accessed | tf_op | source)
XLA Modules:
  0.0 157.3 jit_solution(7549396520795807124)
XLA Ops:
  1.3 0.0 copy-start
  1.3 2.5 %copy-done = bf16[64,64,576]{2,1,0:T(8,128)(2,1)S(1)} copy-done((bf16[64,64,576]{2,1,0:T(8,128)(2,1)S(1)}, bf16[64,64,576]{2,1,0:T(8,128)(2,1)}, u32[]{:S(2)}) %copy-start) | copy-done | bytes 4718616
  3.8 0.0 copy-start.2
  3.8 0.7 copy-done.2
  4.4 0.0 copy-start.3
  4.4 0.7 copy-done.3
  5.1 14.3 %flatten.1 = bf16[16,2,8,18432]{3,2,1,0:T(8,128)(2,1)} custom-call(s32[32]{0:T(128)S(1)} %copy-done.2, s32[32]{0:T(128)S(1)} %copy-done.3, s32[1]{0:T(128)S(6)} %copy.9.count_ref, bf16[64,64,576]{2,1,0:T(8,128)(2,1)S(1)} %copy-done), custom_call_target="tpu_custom_call" | custom-call | tf_op jit(solution)/shard_map/flatten/pallas_call | solution.py:59
  19.4 115.0 %all_to_all.5 = bf16[32,8,18432]{2,1,0:T(8,128)(2,1)S(1)} all-to-all(bf16[32,8,18432]{2,1,0:T(8,128)(2,1)} %bitcast.5), channel_id=1, replica_groups=mesh['own'=32,'rep'=4] {'own'}, dimensions={0} | all-to-all | bytes 18874368 | tf_op jit(solution)/shard_map/all_to_all | solution.py:211
  134.3 6.1 %peak_steps.1.steps_ref = f32[1,288]{1,0:T(1,128)S(1)} custom-call(bf16[256,18432]{1,0:T(8,128)(2,1)S(1)} %bitcast.3), custom_call_target="tpu_custom_call" | custom-call | tf_op jit(solution)/shard_map/peak_steps/pallas_call | solution.py:137
  140.5 8.0 %encode.1 = (bf16[256,18432]{1,0:T(8,128)(2,1)}, f32[1,384]{1,0:T(1,128)S(1)}) custom-call(bf16[256,18432]{1,0:T(8,128)(2,1)S(1)} %bitcast.4, f32[1,288]{1,0:T(1,128)S(1)} %peak_steps.1.steps_ref), custom_call_target="tpu_custom_call" | custom-call | tf_op jit(solution)/shard_map/encode/pallas_call | solution.py:197
  148.5 0.0 copy-start.1
  148.5 0.6 copy-done.1
  149.0 6.4 %error_mean.1 = f32[1,288]{1,0:T(1,128)} custom-call(f32[1,384]{1,0:T(1,128)} %copy-done.1), custom_call_target="tpu_custom_call" | custom-call | tf_op jit(solution)/shard_map/error_mean/pallas_call | solution.py:157
  155.5 0.6 copy.10
  156.0 1.2 copy.11
Async XLA Ops:
  1.3 2.5 %copy-start = (bf16[64,64,576]{2,1,0:T(8,128)(2,1)S(1)}, bf16[64,64,576]{2,1,0:T(8,128)(2,1)}, u32[]{:S(2)}) copy-start(bf16[64,64,576]{2,1,0:T(8,128)(2,1)} %pool_ref.1) | copy-start | bytes 14155780
  3.8 0.7 copy-start.2
  4.4 0.7 copy-start.3
  148.5 0.6 copy-start.1
